TPU v7x, 32 devices: a whole 2x2x4 slice. The times are simulated.
32 devices in a mesh: grp: 4 (over y, x), dev: 8 (over z, core).
Axes of the slice: x: 2, y: 2, z: 4, core: 2. Of those that a mesh axis runs over, the one named last changes fastest.
Arguments:
- pool_rows: bfloat16 [32768, 1024], P(('grp', 'dev')), may hold values from -6 to 6
- sample_index: int32 [32768], P(('grp', 'dev')), may hold values from 0 to 32767, as said below
- cluster_id: int32 [32768], P(('grp', 'dev')), may hold values from 0 to 63, as said below
- child_id: int32 [32768], P(('grp', 'dev')), may hold values from 0 to 7
- old_centroids: float32 [64, 8, 1024], P('dev'), may hold values from -6 to 6
Outputs:
- centroids: float32 [64, 8, 1024], P('dev')
- child_counts: int32 [64, 8], P('dev')
Inputs may be any that keep to these rules, and one draw needn't show every extreme that they name: Sample i takes a pool row of its own aligned block of 1024 rows: sample_index[i] // 1024 == i // 1024. `cluster_id`: in each aligned block of 1024 samples (the rows of one device) the 2 clusters o * 2 to o * 2 + 1 of any owner o are named at most 64 times together, and one cluster, the same in every block, is named exactly 64 times in every block.
All inputs are finite; a program needn't handle non-finite values.
Results may differ from a plain program's by a relative error of at most 0.0003.
Values may be sent and summed in bfloat16 or wider, within the bound.
A program may use at most 64 MiB of HBM per device.

v0:
```python
import functools

import jax
import jax.numpy as jnp
from jax import lax
from jax.experimental import pallas as pl
from jax.experimental.pallas import tpu as pltpu
from jax.sharding import PartitionSpec as P

MESH = pl.DeviceIdType.MESH
LANES = 128
PAIR = 256
BLOCK_ROWS = 256
ROUTES = (("h", "xy", "l"), ("x", "lh", "y"), ("y", "lh", "x"), ("l", "xy", "h"), ("x", "y", "lh"), ("l", "xy", "h"), ("y", "x", "lh"), ("xy", "lh"))
TAKES = ((1, 0), (2, 0), (3, 0), (4, 0), (6, 0), (0, 0), (5, 0), (7, 0), (3, 1), (4, 1), (6, 1), (1, 1), (0, 1), (2, 1), (5, 1), (1, 2), (7, 1), (3, 2), (0, 2), (2, 2), (4, 2), (6, 2), (5, 2))


def log2(n):
    assert n & (n - 1) == 0
    return n.bit_length() - 1


def run(count, body):
    if count == 1:
        body(0)
    else:
        lax.fori_loop(0, count, lambda i, c: (body(i), c)[1], 0)


class Plan:
    def __init__(self, groups, devs, held, kinds, rows, width):
        self.groups, self.devs, self.held, self.kinds = groups, devs, held, kinds
        self.rows, self.width = rows, width
        self.clusters = devs * held
        self.own = held // groups
        self.dev_bits, self.grp_bits = log2(devs), log2(groups)
        self.free_bits = log2(self.own)
        self.bits = log2(self.clusters)
        self.steps = self.dev_bits + self.grp_bits
        self.chunks = width // LANES
        letters = {"x": ("grp", 0), "y": ("grp", 1), "l": ("dev", 1), "h": ("dev", 2)}
        core = (("dev", 0),)
        rest = [(("dev", b),) for b in range(3, self.dev_bits)]
        rest += [(("grp", b),) for b in range(2, self.grp_bits)]
        self.order, self.ends = [], []
        for k in range(self.chunks):
            near = [tuple(letters[c] for c in word) for word in ROUTES[k % len(ROUTES)]]
            self.order.append([core] + near + rest)
        self.takes = [(k, 0) for k in range(self.chunks)]
        for start in range(0, self.chunks, len(ROUTES)):
            self.takes += [(start + k, s + 1) for k, s in TAKES if start + k < self.chunks]
        for s in range(len(rest)):
            self.takes += [(k, len(self.order[k]) - len(rest) + s) for k in range(self.chunks)]
        self.base = [item for group in self.order[0] for item in group]
        self.count_order = [core, (("dev", 1), ("dev", 2))]
        self.count_order += [(("dev", b),) for b in range(3, self.dev_bits)]
        self.pieces = max(sum((1 << len(g)) - 1 for g in o) for o in self.order)
        self.count_pieces = sum((1 << len(g)) - 1 for g in self.count_order)

    def cluster_bit(self, item):
        axis, b = item
        return b + (log2(self.held) if axis == "dev" else self.free_bits)

    def moves(self, order):
        order = [item for group in order for item in group]
        where = {item: self.bits - 1 - s for s, item in enumerate(self.base)}
        there = {item: self.bits - 1 - s for s, item in enumerate(order)}
        return [(where[i], there[i]) for i in order] + [(b, b) for b in range(self.free_bits)]


def permute(value, moves):
    total = 0
    for a, b in moves:
        total = total + ((value // (1 << a)) % 2) * (1 << b)
    return total


def kernel(plan, idx_ref, clu_ref, chi_ref, pool_hbm, old_hbm, out_ref, cnt_ref,
           pool, old, ihot, a_buf, buf, recv, cbuf, crecv, cex, ag,
           load_sem, send_sem, recv_sem, csend_sem, crecv_sem, ag_send, ag_recv):
    p = plan
    grp, dev = lax.axis_index("grp"), lax.axis_index("dev")

    load_pool = pltpu.make_async_copy(pool_hbm, pool, load_sem.at[0])
    load_pool.start()
    load_old = pltpu.make_async_copy(old_hbm, old, load_sem.at[1])
    load_old.start()

    def flip(index, b):
        return index + (1 << b) - 2 * (1 << b) * ((index // (1 << b)) % 2)

    def partner(group, mask):
        g, d = grp, dev
        for at, (axis, b) in enumerate(reversed(group)):
            if (mask >> at) & 1:
                g, d = (g, flip(d, b)) if axis == "dev" else (flip(g, b), d)
        return (g, d)

    def mate(o):
        other = grp
        for b in range(p.grp_bits):
            if (o >> b) & 1:
                other = flip(other, b)
        return (other, dev)

    named = {}
    for order in p.order + [p.count_order, [tuple(("grp", b) for b in range(p.grp_bits))]]:
        for group in order:
            for mask in range(1, 1 << len(group)):
                picked = [i for at, i in enumerate(reversed(group)) if (mask >> at) & 1]
                named[tuple(sorted(picked))] = (group, mask)
    greeted = [partner(*named[name]) for name in sorted(named)]
    barrier = pltpu.get_barrier_semaphore()
    for other in greeted:
        pl.semaphore_signal(barrier, inc=1, device_id=other, device_id_type=MESH)

    local = idx_ref[...] - (grp * p.devs + dev) * p.rows
    cluster = clu_ref[...]
    child = chi_ref[...]
    relative = jnp.bitwise_xor(cluster, dev * p.held + grp * p.own)

    def label(pairs):
        total = None
        for a, b in pairs:
            term = (lax.shift_right_logical(relative, a) & 1) << b
            total = term if total is None else total + term
        return total

    base_pairs = [(p.cluster_bit(i), p.bits - 1 - s) for s, i in enumerate(p.base)]
    base_pairs += [(b, b) for b in range(p.free_bits)]
    segment = label(base_pairs) * p.kinds + child

    def onehot(rows, start, labels):
        at = lax.broadcasted_iota(jnp.int32, (rows, p.rows), 0) + start
        return jnp.where(at == labels, 1.0, 0.0).astype(jnp.bfloat16)

    def dot_t(a, b):
        return lax.dot_general(a, b, (((1,), (1,)), ((), ())), preferred_element_type=jnp.float32)

    log_held = log2(p.held)
    count_label = label(
        [(log_held + b, p.dev_bits - 1 - s + log_held) for s, (_, b) in
         enumerate([i for g in p.count_order for i in g])]
    ) + cluster % p.held
    hits = dot_t(onehot(p.clusters, 0, count_label), onehot(LANES, 0, child))
    cbuf[...] = hits.reshape(p.devs, p.held, LANES)

    def exchange(src, dst, s_sem, r_sem, device):
        return pltpu.make_async_remote_copy(
            src_ref=src, dst_ref=dst, send_sem=s_sem, recv_sem=r_sem,
            device_id=device, device_id_type=MESH)

    def parts(order, total, s):
        before = sum(len(g) for g in order[:s])
        first = sum((1 << len(g)) - 1 for g in order[:s]) - 1
        n = (total >> before) >> len(order[s])
        return [(m, m * n, n, first + m) for m in range(1, 1 << len(order[s]))]

    def pieces(k, s):
        got = []
        for m, at, n, sem in parts(p.order[k], p.clusters, s):
            span = pl.ds(at, n)
            got.append(exchange(buf.at[k, span], recv.at[k, span], send_sem.at[k, sem],
                                recv_sem.at[k, sem], partner(p.order[k][s], m)))
        return got

    def count_pieces(s):
        if s == len(p.count_order):
            return [exchange(cbuf.at[0], cex.at[o - 1], csend_sem.at[p.count_pieces + o - 1],
                             crecv_sem.at[p.count_pieces + o - 1], mate(o))
                    for o in range(1, p.groups)]
        got = []
        for m, at, n, sem in parts(p.count_order, p.devs, s):
            span = pl.ds(at, n)
            got.append(exchange(cbuf.at[span], crecv.at[span], csend_sem.at[sem],
                                crecv_sem.at[sem], partner(p.count_order[s], m)))
        return got

    def start(copies):
        for copy in copies:
            copy.start()

    def take_count(s):
        for copy in count_pieces(s):
            copy.wait_recv()
        todo = parts(p.count_order, p.devs, s)
        n = todo[0][2]
        total = cbuf[0:n]
        for _, at, n, _ in todo:
            total = total + crecv[at:at + n]
        cbuf[0:n] = total
        start(count_pieces(s + 1))

    mine = pl.ds(grp * p.own, p.own)

    def gather(k):
        return [exchange(buf.at[k, 0:p.own], ag.at[k, mine], ag_send.at[k, o - 1],
                         ag_recv.at[k, o - 1], mate(o)) for o in range(1, p.groups)]

    def take(k, s):
        for copy in pieces(k, s):
            copy.wait_recv()
        todo = parts(p.order[k], p.clusters, s)
        n = todo[0][2]
        total = buf[k, 0:n]
        for _, at, n, _ in todo:
            total = total + recv[k, at:at + n]
        buf[k, 0:n] = total
        if s + 1 < len(p.order[k]):
            start(pieces(k, s + 1))
        else:
            start(gather(k))
            ag[k, mine] = total

    ihot[...] = onehot(p.rows, 0, local)
    half_rows = p.clusters * p.kinds // 2
    block = min(BLOCK_ROWS, half_rows)
    blocks = half_rows // block
    block_clusters = block // p.kinds

    for half in (1, 0):

        def rows_of(i):
            return pl.ds(i * block, block)

        def make_a(i):
            hot = onehot(block, half * half_rows + i * block, segment)
            a_buf[rows_of(i), :] = dot_t(hot, ihot[...]).astype(jnp.bfloat16)

        run(blocks, make_a)
        if half == 1:
            load_pool.wait()
        for c in range(p.width // PAIR):

            def multiply(i):
                got = jnp.dot(a_buf[rows_of(i), :], pool[:, c * PAIR:(c + 1) * PAIR],
                              preferred_element_type=jnp.float32)
                got = got.reshape(block_clusters, p.kinds, PAIR)
                for q in range(PAIR // LANES):
                    k = c * (PAIR // LANES) + q
                    moves = p.moves(p.order[k])
                    start = permute((half * half_rows + i * block) // p.kinds, moves)
                    for j in range(block_clusters):
                        buf[k, start + permute(j, moves)] = got[j, :, q * LANES:(q + 1) * LANES]

            run(blocks, multiply)
            if half == 1:
                if c == 0:
                    pl.semaphore_wait(barrier, len(greeted))
                for q in range(PAIR // LANES):
                    start(pieces(c * (PAIR // LANES) + q, 0))

    start(count_pieces(0))
    due = {p.chunks - 1: 0}
    for s in range(1, len(p.count_order)):
        due[len(p.takes) // 2 + s - 1] = s
    for at, (k, s) in enumerate(p.takes):
        take(k, s)
        if at in due:
            take_count(due[at])

    last = len(p.count_order)
    for copy in count_pieces(last):
        copy.wait_recv()
    total = cbuf[0]
    for o in range(1, p.groups):
        total = total + cex[o - 1]
    cnt_ref[...] = total[:, 0:p.kinds].astype(jnp.int32)
    pick = (lax.broadcasted_iota(jnp.int32, (p.held, p.kinds, LANES), 1)
            == lax.broadcasted_iota(jnp.int32, (p.held, p.kinds, LANES), 2))
    spread = jnp.where(pick, total[:, None, :], 0.0)
    divisor = jnp.sum(spread, axis=2, keepdims=True) + 1.0
    load_old.wait()

    ends = [k for k, s in p.takes if s == len(p.order[k]) - 1]
    for k in ends:
        for o in range(1, p.groups):
            theirs = pl.ds(mate(o)[0] * p.own, p.own)
            exchange(buf.at[k, 0:p.own], ag.at[k, theirs], ag_send.at[k, o - 1],
                     ag_recv.at[k, o - 1], mate(o)).wait_recv()
        lanes = slice(k * LANES, (k + 1) * LANES)
        out_ref[:, :, lanes] = (ag[k] + old[:, :, lanes]) / divisor

    for k in range(p.chunks):
        for s in range(len(p.order[k])):
            for copy in pieces(k, s):
                copy.wait_send()
        for copy in gather(k):
            copy.wait_send()
    for s in range(last + 1):
        for copy in count_pieces(s):
            copy.wait_send()


def finish(centroids, counts):
    def body(a_ref, b_ref, c_ref, d_ref):
        c_ref[...] = a_ref[...]
        d_ref[...] = b_ref[...]

    whole = pl.BlockSpec(memory_space=pltpu.VMEM)
    shapes = [jax.ShapeDtypeStruct(a.shape, a.dtype) for a in (centroids, counts)]
    return pl.pallas_call(body, out_shape=tuple(shapes), in_specs=[whole, whole],
                          out_specs=(whole, whole))(centroids, counts)


def per_device(groups, devs, pool_rows, sample_index, cluster_id, child_id, old_centroids):
    rows, width = pool_rows.shape
    held, kinds, _ = old_centroids.shape
    plan = Plan(groups, devs, held, kinds, rows, width)
    f32, bf16 = jnp.float32, jnp.bfloat16
    whole = pl.BlockSpec(memory_space=pltpu.VMEM)
    stay = pl.BlockSpec(memory_space=pl.ANY)
    half_rows = plan.clusters * kinds // 2
    return finish(*pl.pallas_call(
        functools.partial(kernel, plan),
        out_shape=(
            jax.ShapeDtypeStruct((held, kinds, width), f32),
            jax.ShapeDtypeStruct((held, kinds), jnp.int32),
        ),
        in_specs=[whole, whole, whole, stay, stay],
        out_specs=(whole, whole),
        scratch_shapes=[
            pltpu.VMEM((rows, width), bf16),
            pltpu.VMEM((held, kinds, width), f32),
            pltpu.VMEM((rows, rows), bf16),
            pltpu.VMEM((half_rows, rows), bf16),
            pltpu.VMEM((plan.chunks, plan.clusters, kinds, LANES), f32),
            pltpu.VMEM((plan.chunks, plan.clusters, kinds, LANES), f32),
            pltpu.VMEM((devs, held, LANES), f32),
            pltpu.VMEM((devs, held, LANES), f32),
            pltpu.VMEM((groups - 1, held, LANES), f32),
            pltpu.VMEM((plan.chunks, held, kinds, LANES), f32),
            pltpu.SemaphoreType.DMA((2,)),
            pltpu.SemaphoreType.DMA((plan.chunks, plan.pieces)),
            pltpu.SemaphoreType.DMA((plan.chunks, plan.pieces)),
            pltpu.SemaphoreType.DMA((plan.count_pieces + groups - 1,)),
            pltpu.SemaphoreType.DMA((plan.count_pieces + groups - 1,)),
            pltpu.SemaphoreType.DMA((plan.chunks, groups - 1)),
            pltpu.SemaphoreType.DMA((plan.chunks, groups - 1)),
        ],
        compiler_params=pltpu.CompilerParams(
            collective_id=0, has_side_effects=True, vmem_limit_bytes=60 * 2**20
        ),
    )(
        sample_index.reshape(1, rows),
        cluster_id.reshape(1, rows),
        child_id.reshape(1, rows),
        pool_rows,
        old_centroids,
    ))


def solution(mesh):
    placed = (
        P(("grp", "dev"), None),
        P(("grp", "dev")),
        P(("grp", "dev")),
        P(("grp", "dev")),
        P("dev", None, None),
    )
    return jax.shard_map(
        functools.partial(per_device, mesh.shape["grp"], mesh.shape["dev"]),
        mesh=mesh,
        in_specs=placed,
        out_specs=(P("dev", None, None), P("dev", None)),
        check_vma=False,
    )
```

profile of v0, /device:TPU:0, one launch (start us, length us, event | category | flops | bytes accessed | tf_op | source)
XLA Modules:
  0.0 30.0 jit_solution(10850012521168953035)
XLA Ops:
  0.6 27.7 %shard_map.68 = (f32[8,8,1024]{2,1,0:T(8,128)}, s32[8,8]{1,0:T(8,128)}) custom-call(s32[1,1024]{1,0:T(1,128)} %bitcast.3, s32[1,1024]{1,0:T(1,128)} %bitcast.4, s32[1,1024]{1,0:T(1,128)} %bitcast.5, bf16[1024,1024]{1,0:T(8,128)(2,1)} %pool_hbm.1, f32[8,8,1024]{2,1,0:T(8,128)} %old_hbm.1), custom_call_target="tpu_custom_call" | custom-call | tf_op jit(solution)/shard_map/pallas_call | solution.py:314
  28.4 1.7 %shard_map.69 = (f32[8,8,1024]{2,1,0:T(8,128)}, s32[8,8]{1,0:T(8,128)}) custom-call(f32[8,8,1024]{2,1,0:T(8,128)} %get-tuple-element.4.a_ref, s32[8,8]{1,0:T(8,128)} %get-tuple-element.5.b_ref), custom_call_target="tpu_custom_call" | custom-call | tf_op jit(solution)/shard_map/pallas_call | solution.py:302
where the time goes:
time: 30.2 us; the launch traced here: 30 us
  Pallas kernels  29.4 us (97%)
  between operations  0.64 us (2%)
    pallas_call x1, Pallas kernels, per_device(): pl.pallas_call(functools.partial(kernel, plan), out_shape=(jax.ShapeDtype...  27.7 us
    pallas_call x1, Pallas kernels, finish(): pl.pallas_call(body, out_shape=tuple(shapes), in_specs=[whole, whole], ou...  1.68 us

commit v1 on v0

--- a/solution.py
+++ b/solution.py
@@ -75,12 +75,16 @@
     return total
 
 
-def kernel(plan, idx_ref, clu_ref, chi_ref, pool_hbm, old_hbm, out_ref, cnt_ref,
-           pool, old, ihot, a_buf, buf, recv, cbuf, crecv, cex, ag,
+def kernel(plan, idx_hbm, clu_hbm, chi_hbm, pool_hbm, old_hbm, out_ref, cnt_ref,
+           idx_ref, clu_ref, chi_ref, id_sem, pool, old, ihot, a_buf, buf, recv, cbuf, crecv, cex, ag,
            load_sem, send_sem, recv_sem, csend_sem, crecv_sem, ag_send, ag_recv):
     p = plan
     grp, dev = lax.axis_index("grp"), lax.axis_index("dev")
 
+    pairs = ((idx_hbm, idx_ref), (clu_hbm, clu_ref), (chi_hbm, chi_ref))
+    ids = [pltpu.make_async_copy(a, b, id_sem.at[i]) for i, (a, b) in enumerate(pairs)]
+    for c in ids:
+        c.start()
     load_pool = pltpu.make_async_copy(pool_hbm, pool, load_sem.at[0])
     load_pool.start()
     load_old = pltpu.make_async_copy(old_hbm, old, load_sem.at[1])
@@ -114,6 +118,8 @@
     for other in greeted:
         pl.semaphore_signal(barrier, inc=1, device_id=other, device_id_type=MESH)
 
+    for c in ids:
+        c.wait()
     local = idx_ref[...] - (grp * p.devs + dev) * p.rows
     cluster = clu_ref[...]
     child = chi_ref[...]
@@ -300,7 +306,7 @@
     whole = pl.BlockSpec(memory_space=pltpu.VMEM)
     shapes = [jax.ShapeDtypeStruct(a.shape, a.dtype) for a in (centroids, counts)]
     return pl.pallas_call(body, out_shape=tuple(shapes), in_specs=[whole, whole],
-                          out_specs=(whole, whole))(centroids, counts)
+                          out_specs=(whole, whole), compiler_params=pltpu.CompilerParams(vmem_limit_bytes=4 * 2**20))(centroids, counts)
 
 
 def per_device(groups, devs, pool_rows, sample_index, cluster_id, child_id, old_centroids):
@@ -309,7 +315,7 @@
     plan = Plan(groups, devs, held, kinds, rows, width)
     f32, bf16 = jnp.float32, jnp.bfloat16
     whole = pl.BlockSpec(memory_space=pltpu.VMEM)
-    stay = pl.BlockSpec(memory_space=pl.ANY)
+    stay = pl.BlockSpec(memory_space=pltpu.HBM)
     half_rows = plan.clusters * kinds // 2
     return finish(*pl.pallas_call(
         functools.partial(kernel, plan),
@@ -317,9 +323,13 @@
             jax.ShapeDtypeStruct((held, kinds, width), f32),
             jax.ShapeDtypeStruct((held, kinds), jnp.int32),
         ),
-        in_specs=[whole, whole, whole, stay, stay],
+        in_specs=[stay, stay, stay, stay, stay],
         out_specs=(whole, whole),
         scratch_shapes=[
+            pltpu.VMEM((1, rows), jnp.int32),
+            pltpu.VMEM((1, rows), jnp.int32),
+            pltpu.VMEM((1, rows), jnp.int32),
+            pltpu.SemaphoreType.DMA((3,)),
             pltpu.VMEM((rows, width), bf16),
             pltpu.VMEM((held, kinds, width), f32),
             pltpu.VMEM((rows, rows), bf16),
@@ -339,14 +349,10 @@
             pltpu.SemaphoreType.DMA((plan.chunks, groups - 1)),
         ],
         compiler_params=pltpu.CompilerParams(
-            collective_id=0, has_side_effects=True, vmem_limit_bytes=60 * 2**20
+            collective_id=0, has_side_effects=True, vmem_limit_bytes=50 * 2**20
         ),
     )(
-        sample_index.reshape(1, rows),
-        cluster_id.reshape(1, rows),
-        child_id.reshape(1, rows),
-        pool_rows,
-        old_centroids,
+        *[pltpu.with_memory_space_constraint(a, pltpu.HBM) for a in (sample_index.reshape(1, rows), cluster_id.reshape(1, rows), child_id.reshape(1, rows), pool_rows, old_centroids)],
     ))
 
 

time: 30.2 us -> 28.2 us (0.934)
  Pallas kernels: 29.4 us -> 27.3 us
    pallas_call x1, Pallas kernels: 27.7 us -> 26.6 us  [per_device(): pl.pallas_call(functools.partial(kernel, plan), out_shape=(jax.ShapeDtype...]
    pallas_call x1, Pallas kernels: 1.68 us -> 0.72 us  [finish(): pl.pallas_call(body, out_shape=tuple(shapes), in_specs=[whole, whole], ou...]
where the time goes in v1:
time: 28.2 us; the launch traced here: 28 us
  Pallas kernels  27.3 us (97%)
  between operations  0.64 us (2%)
    pallas_call x1, Pallas kernels, per_device(): pl.pallas_call(functools.partial(kernel, plan), out_shape=(jax.ShapeDtype...  26.6 us
    pallas_call x1, Pallas kernels, finish(): pl.pallas_call(body, out_shape=tuple(shapes), in_specs=[whole, whole], ou...  0.72 us

profile of v1, /device:TPU:0, one launch (start us, length us, event | category | flops | bytes accessed | tf_op | source)
XLA Modules:
  0.0 28.0 jit_solution(9906141365857129746)
XLA Ops:
  0.6 26.6 %shard_map.68 = (f32[8,8,1024]{2,1,0:T(8,128)S(1)}, s32[8,8]{1,0:T(8,128)S(1)}) custom-call(s32[1,1024]{1,0:T(1,128)} %bitcast.3, s32[1,1024]{1,0:T(1,128)} %bitcast.4, s32[1,1024]{1,0:T(1,128)} %bitcast.5, bf16[1024,1024]{1,0:T(8,128)(2,1)} %pool_hbm.1, f32[8,8,1024]{2,1,0:T(8,128)} %old_hbm.1), custom_call_target="tpu_custom_call" | custom-call | tf_op jit(solution)/shard_map/pallas_call | solution.py:320
  27.3 0.7 %shard_map.69 = (f32[8,8,1024]{2,1,0:T(8,128)}, s32[8,8]{1,0:T(8,128)}) custom-call(f32[8,8,1024]{2,1,0:T(8,128)S(1)} %get-tuple-element.4.a_ref, s32[8,8]{1,0:T(8,128)S(1)} %get-tuple-element.5.b_ref), custom_call_target="tpu_custom_call" | custom-call | tf_op jit(solution)/shard_map/pallas_call | solution.py:308
